TPU v7x, 256 devices: a whole 4x4x8 slice. The times are simulated.
256 devices in a mesh: section: 8 (over y, core), mp: 32 (over x, z).
Axes of the slice: x: 4, y: 4, z: 8, core: 2. Of those that a mesh axis runs over, the one named last changes fastest.
Arguments:
- arriving: bfloat16 [8, 768, 8192], P('section', None, 'mp'), may hold values from -6 to 6
- norm_gain: bfloat16 [8, 8192], P('section'), may hold values from 0.099609375 to 1.8984375
- w_query: bfloat16 [8, 8192, 8192], P('section', 'mp'), may hold values from -26 to 26
- w_key: bfloat16 [8, 1024, 8192], P('section', 'mp'), may hold values from -1 to 1
- w_value: bfloat16 [8, 1024, 8192], P('section', 'mp'), may hold values from -0.25 to 0.25
- w_out: bfloat16 [8, 8192, 8192], P('section', 'mp'), may hold values from -0.0625 to 0.0625
Outputs:
- attended: bfloat16 [8, 768, 8192], P('section', 'mp')
- stream_next: bfloat16 [8, 768, 8192], P('section', 'mp')
All inputs are finite; a program needn't handle non-finite values.
Results may differ from a plain program's by a relative error of at most 0.017.
Values may be sent and summed in bfloat16 or wider, within the bound.
A program may use at most 128 MiB of HBM per device.

v0:
```python
import math
import jax
import jax.numpy as jnp
from jax import lax
from jax.sharding import Mesh
from jax.sharding import PartitionSpec as P

HD = 128
KV_HEADS = 8
MP = ("mp_0", "mp_1")
rope_base = 500000.0
norm_eps = 1e-05


def shifted(block, axis, distance):
    devices = range(lax.axis_size(axis))
    route = [((i - distance) % len(devices), i) for i in devices]
    return lax.ppermute(block, axis, route)


def sent_together(arrays, axis, dim, along):
    both = jnp.concatenate(arrays, axis=along)
    result, at, outs = (lax.all_gather(both, axis, axis=dim, tiled=True), 0, [])
    for a in arrays:
        outs.append(lax.slice_in_dim(result, at, at + a.shape[along], axis=along))
        at += a.shape[along]
    return tuple(outs)


def scatter_axes(array, axes, dim):
    for axis in axes:
        array = lax.psum_scatter(array, axis, scatter_dimension=dim, tiled=True)
    return array


def rotate_pairs(channel_major, pair_ids):
    channels = channel_major.shape[0]
    length = channel_major.shape[1]
    frequency = jnp.exp(pair_ids.astype(jnp.float32) * (-2.0 * math.log(rope_base) / HD))
    positions = jnp.arange(length, dtype=jnp.int32).astype(jnp.float32)
    angles = frequency[:, None] * positions[None, :]
    cos_table = jnp.cos(angles)
    sine_table = jnp.sin(angles)
    paired = channel_major.reshape(channels // 2, 2, length)
    even_part = paired[:, 0]
    odd_part = paired[:, 1]
    rotated = jnp.stack(
        [
            even_part * cos_table - odd_part * sine_table,
            even_part * sine_table + odd_part * cos_table,
        ],
        axis=1,
    )
    return rotated.reshape(channels, length)


def head_rows(table, kv_index):
    length = table.shape[1]
    grouped = table.reshape(HD // 2, KV_HEADS, 2, length)
    picked = lax.dynamic_slice_in_dim(grouped, kv_index, 1, 1)
    return picked.reshape(HD, length)


def normalize(hidden_in, gain_row):
    as_float = hidden_in.astype(jnp.float32)
    mean_square = jnp.mean(as_float * as_float, axis=1, keepdims=True)
    normed = (as_float * lax.rsqrt(mean_square + norm_eps) * gain_row).astype(jnp.bfloat16)
    return (as_float, normed)


def channel_product(weights, normed):
    return lax.dot_general(
        weights, normed, (((1,), (1,)), ((), ())), preferred_element_type=jnp.float32
    )


def local(arriving, norm_gain, w_query, w_key, w_value, w_out):
    local_block = arriving[0]
    gain_row = norm_gain[0].astype(jnp.float32)
    query_weights = w_query[0]
    key_weights = w_key[0]
    value_weights = w_value[0]
    out_weights = w_out[0]
    mp_count = lax.axis_size(MP)
    member = lax.axis_index(MP)
    length = local_block.shape[0]
    row_count = length // mp_count
    arrived = shifted(local_block, "section", 1)
    whole_rows = lax.all_gather(arrived, MP, axis=1, tiled=True)
    full_float, normed_all = normalize(whole_rows, gain_row)
    residual = lax.dynamic_slice_in_dim(full_float, member * row_count, row_count, 0)
    projected = jnp.concatenate(
        [
            channel_product(query_weights, normed_all),
            channel_product(key_weights, normed_all),
            channel_product(value_weights, normed_all),
        ],
        axis=0,
    )
    q_width = query_weights.shape[0]
    k_width = key_weights.shape[0]
    query_pairs = jnp.arange(q_width // 2, dtype=jnp.int32) * 2 % HD // 2
    query_part = rotate_pairs(projected[:q_width], query_pairs).astype(jnp.bfloat16)
    key_pairs = (member * k_width + jnp.arange(k_width // 2, dtype=jnp.int32) * 2) // (2 * KV_HEADS)
    key_part = rotate_pairs(projected[q_width : q_width + k_width], key_pairs).astype(jnp.bfloat16)
    value_part = projected[q_width + k_width :].astype(jnp.bfloat16)
    key_all, value_all = sent_together((key_part, value_part), MP, 0, 1)
    local_heads = q_width // HD
    group_size = local_heads * mp_count // KV_HEADS
    kv_index = member * local_heads // group_size
    key_head = head_rows(key_all, kv_index)
    value_head = head_rows(value_all, kv_index)
    query_heads = query_part.reshape(local_heads, HD, length)
    score_scale = 1.0 / math.sqrt(HD)
    scores = (
        jnp.einsum("hdi,dj->hij", query_heads, key_head, preferred_element_type=jnp.float32)
        * score_scale
    )
    token_index = jnp.arange(length, dtype=jnp.int32)
    causal = token_index[:, None] >= token_index[None, :]
    scores = jnp.where(causal[None], scores, -1e30)
    row_max = jnp.max(scores, axis=-1, keepdims=True)
    exponent = jnp.exp(scores - row_max)
    row_total = jnp.sum(exponent, axis=-1, keepdims=True)
    weights = (exponent / row_total).astype(jnp.bfloat16)
    context = jnp.einsum(
        "hij,dj->ihd", weights, value_head, preferred_element_type=jnp.float32
    ).astype(jnp.bfloat16)
    context = context.reshape(length, q_width)
    full_term = jnp.dot(context, out_weights, preferred_element_type=jnp.float32)
    summed = scatter_axes(full_term.astype(jnp.bfloat16), MP, 0).astype(jnp.float32)
    attended = summed.astype(jnp.bfloat16)[None]
    stream_next = (residual + summed).astype(jnp.bfloat16)[None]
    return (attended, stream_next)


def solution(mesh):
    finer = Mesh(mesh.devices.reshape(mesh.shape["section"], 4, 8), ("section", "mp_0", "mp_1"))
    return jax.shard_map(
        local,
        mesh=finer,
        in_specs=(
            P("section", None, MP),
            P("section", None),
            P("section", MP, None),
            P("section", MP, None),
            P("section", MP, None),
            P("section", MP, None),
        ),
        out_specs=(P("section", MP, None), P("section", MP, None)),
        check_vma=False,
    )
```

profile of v0, /device:TPU:6, one launch (start us, length us, event | category | flops | bytes accessed | tf_op | source)
XLA Modules:
  0.0 442.5 jit_solution(10435901316648829320)
XLA Ops:
  7.3 8.6 %collective-permute-done = bf16[768,256]{1,0:T(8,128)(2,1)S(1)} collective-permute-done((bf16[768,256]{1,0:T(8,128)(2,1)}, bf16[768,256]{1,0:T(8,128)(2,1)S(1)}, u32[]{:S(2)}, u32[]{:S(2)}) %collective-permute-start) | collective-permute-done | bytes 393248 | tf_op jit(solution)/shard_map/ppermute | solution.py:18
  15.9 0.7 copy-done.5
  16.7 0.8 mul.219
  17.5 125.5 %all-gather.3.cloned.1.call-done = bf16[768,8192]{1,0:T(8,128)(2,1)} async-done(((bf16[768,256]{1,0:T(8,128)(2,1)}), bf16[768,8192]{1,0:T(8,128)(2,1)}) %all-gather.3.cloned.1.call-update) | async-done | bytes 12582928 | tf_op jit(solution)/shard_map/all_gather | solution.py:89
  143.0 7.1 %multiply_reduce_fusion = f32[768]{0:T(1024)S(1)} fusion(bf16[768,8192]{1,0:T(8,128)(2,1)} %all-gather.3.cloned.1.call-done), kind=kLoop, calls=%fused_computation.2 | loop fusion | flops 18873600 | bytes 12585984 | tf_op jit(solution)/shard_map/reduce_sum | solution.py:66
  150.1 7.5 %multiply_convert_fusion = bf16[768,8192]{1,0:T(8,128)(2,1)S(1)} fusion(f32[8192]{0:T(1024)S(1)} %bitcast.54, f32[768]{0:T(1024)S(1)} %add_rsqrt_fusion, bf16[768,8192]{1,0:T(8,128)(2,1)} %all-gather.3.cloned.1.call-done), kind=kLoop, calls=%fused_computation.1 | loop fusion | flops 25165824 | bytes 25201664 | tf_op jit(solution)/shard_map/convert_element_type | solution.py:67
  157.6 3.8 fusion.13
  161.4 0.7 copy-done.2
  162.1 3.8 convolution_bitcast_fusion
  167.4 14.0 %fusion.9 = f32[256,768]{1,0:T(8,128)S(1)} fusion(bf16[768,8192]{1,0:T(8,128)(2,1)} %copy-done.2, bf16[1,256,8192]{2,1,0:T(8,128)(2,1)} %param.8), kind=kOutput, calls=%fused_computation.16 | convolution fusion | flops 3221225472 | bytes 17563648 | tf_op jit(solution)/shard_map/dot_general | solution.py:72
  182.5 1.7 fusion.23
  184.8 58.3 %all-gather.5.cloned.1.call-done = bf16[1024,1536]{1,0:T(8,128)(2,1)} async-done(((bf16[32,1536]{1,0:T(8,128)(2,1)}), bf16[1024,1536]{1,0:T(8,128)(2,1)}) %all-gather.5.cloned.1.call-update) | async-done | bytes 3145744 | tf_op jit(solution)/shard_map/all_gather | solution.py:23
  243.1 3.2 fusion.45
  246.3 4.5 %reshape.285 = bf16[64,8,2,768]{3,2,1,0:T(2,128)(2,1)} reshape(bf16[1024,768]{1,0:T(8,128)(2,1)} %get-tuple-element.2) | data formatting | bytes 3145728 | tf_op jit(solution)/shard_map/reshape | solution.py:59
  250.8 1.1 dynamic-slice_bitcast_fusion
  252.0 1.5 reshape.282
  253.5 1.1 constant_dynamic-slice_fusion
  254.7 3.8 fusion.48
  258.5 3.0 fusion.12
  262.1 6.4 %convolution_convert_fusion = bf16[768,8192]{1,0:T(8,128)(2,1)} fusion(bf16[768,256]{0,1:T(8,128)(2,1)S(1)} %bitcast.53, bf16[1,256,8192]{2,1,0:T(8,128)(2,1)S(1)} %copy-done.3), kind=kOutput, calls=%fused_computation.3 | convolution fusion | flops 3227516928 | bytes 17170432 | tf_op jit(solution)/shard_map/dot_general | solution.py:130
  268.6 113.6 %reduce-scatter.3.cloned.1.call-done = bf16[192,8192]{1,0:T(8,128)(2,1)} async-done(((bf16[768,8192]{1,0:T(8,128)(2,1)}), bf16[192,8192]{1,0:T(8,128)(2,1)}) %reduce-scatter.3.cloned.1.call-update) | async-done | bytes 3145744 | tf_op jit(solution)/shard_map/reduce_scatter | solution.py:32
  382.2 14.2 %convert_element_type.84 = f32[768,8192]{1,0:T(8,128)} convert(bf16[768,8192]{1,0:T(8,128)(2,1)} %all-gather.3.cloned.1.call-done) | non-fusion elementwise | flops 6291456 | bytes 37748736 | tf_op jit(solution)/shard_map/convert_element_type | solution.py:65
  396.4 37.5 %reduce-scatter.5.cloned.1.call-done = bf16[24,8192]{1,0:T(8,128)(2,1)} async-done(((bf16[192,8192]{1,0:T(8,128)(2,1)}), bf16[24,8192]{1,0:T(8,128)(2,1)}) %reduce-scatter.5.cloned.1.call-update) | async-done | bytes 393232 | tf_op jit(solution)/shard_map/reduce_scatter | solution.py:32
  433.9 2.1 fusion.26
  (38 shorter events, 4.1 us)
Async XLA Ops:
  7.2 150.4 %copy-start = (bf16[1,32,8192]{2,1,0:T(8,128)(2,1)S(1)}, bf16[1,32,8192]{2,1,0:T(8,128)(2,1)}, u32[]{:S(2)}) copy-start(bf16[1,32,8192]{2,1,0:T(8,128)(2,1)} %param.10) | copy-start | bytes 1572868
  7.2 135.8 %all-gather.3.cloned.1.call-start = ((), (), s32[]{:S(2)}) async-start(), calls=%async_computation.2 | async-start | bytes 12976128 | tf_op jit(solution)/shard_map/all_gather | solution.py:89
  7.2 8.6 %collective-permute-start = (bf16[768,256]{1,0:T(8,128)(2,1)}, bf16[768,256]{1,0:T(8,128)(2,1)S(1)}, u32[]{:S(2)}, u32[]{:S(2)}) collective-permute-start(bf16[768,256]{1,0:T(8,128)(2,1)} %bitcast.55), channel_id=1, source_target_pairs={{224,0},{0,32},{32,64},{64,96},{96,128},{128,160},{160,192},{192,2... | collective-permute-start | bytes 1179656 | tf_op jit(solution)/shard_map/ppermute | solution.py:18
  15.9 0.7 copy-start.5
  16.6 226.5 %all-gather.5.cloned.1.call-start = ((), (), s32[]{:S(2)}) async-start(), calls=%async_computation.3 | async-start | bytes 3244032 | tf_op jit(solution)/shard_map/all_gather | solution.py:23
  157.6 4.5 %copy-start.2 = (bf16[768,8192]{1,0:T(8,128)(2,1)}, bf16[768,8192]{1,0:T(8,128)(2,1)S(1)}, u32[]{:S(2)}) copy-start(bf16[768,8192]{1,0:T(8,128)(2,1)S(1)} %multiply_convert_fusion) | copy-start | bytes 37748740
  157.6 4.5 %copy-start.4 = (bf16[1,32,8192]{2,1,0:T(8,128)(2,1)S(1)}, bf16[1,32,8192]{2,1,0:T(8,128)(2,1)}, u32[]{:S(2)}) copy-start(bf16[1,32,8192]{2,1,0:T(8,128)(2,1)} %param.9) | copy-start | bytes 1572868
  167.1 215.0 %reduce-scatter.3.cloned.1.call-start = ((), (), s32[]{:S(2)}) async-start(), calls=%async_computation.4 | async-start | bytes 15728640 | tf_op jit(solution)/shard_map/reduce_scatter | solution.py:32
  258.5 3.6 copy-start.3
  268.5 165.4 %reduce-scatter.5.cloned.1.call-start = ((), (), s32[]{:S(2)}) async-start(), calls=%async_computation.5 | async-start | bytes 3538944 | tf_op jit(solution)/shard_map/reduce_scatter | solution.py:32
  382.2 53.8 %copy-start.1 = (bf16[1,32,8192]{2,1,0:T(8,128)(2,1)S(1)}, bf16[1,32,8192]{2,1,0:T(8,128)(2,1)}, u32[]{:S(2)}) copy-start(bf16[1,32,8192]{2,1,0:T(8,128)(2,1)} %param.10) | copy-start | bytes 1572868
Sparse Core Ops, SparseCore 0:
  16.8 126.1 all-gather.2
  167.2 75.8 all-gather.4
  268.6 113.4 reduce-scatter.2
  385.1 48.7 reduce-scatter.4
where the time goes:
time: 443 us
  waiting for transfers between devices  344 us (78%)
  matrix products  34.9 us (8%)
  other arithmetic  34.5 us (8%)
  local copies, waits for them, and re-layouts  15.5 us (3%)
  between operations  14 us (3%)
    reduce_scatter x2, waiting for transfers between devices, scatter_axes(): array = lax.psum_scatter(array, axis, scatter_dimension=dim, tiled=True)  151 us
    all_gather x1, waiting for transfers between devices, local(): whole_rows = lax.all_gather(arrived, MP, axis=1, tiled=True)  125 us
    all_gather x1, waiting for transfers between devices, sent_together(): result, at, outs = (lax.all_gather(both, axis, axis=dim, tiled=True), 0, [])  58.3 us
    dot_general x3, matrix products, channel_product(): lax.dot_general(weights, normed, (((1,), (1,)), ((), ())), preferred_elem...  21.7 us
    convert_element_type x1, other arithmetic, normalize(): as_float = hidden_in.astype(jnp.float32)  14.2 us
  transfers between devices with their start and end apart: 5, of which 5 were waited for; matrix products, arithmetic and copies ran while one was open for 7% of the time, Pallas kernels for 0%

commit v1 on v0

--- a/solution.py
+++ b/solution.py
@@ -86,7 +86,10 @@
     length = local_block.shape[0]
     row_count = length // mp_count
     arrived = shifted(local_block, "section", 1)
-    whole_rows = lax.all_gather(arrived, MP, axis=1, tiled=True)
+    size = lax.axis_size(MP)
+    blocks = jnp.stack([arrived for _ in range(size)])
+    blocks = lax.all_to_all(blocks, MP, split_axis=0, concat_axis=0)
+    whole_rows = jnp.concatenate(blocks, axis=1)
     full_float, normed_all = normalize(whole_rows, gain_row)
     residual = lax.dynamic_slice_in_dim(full_float, member * row_count, row_count, 0)
     projected = jnp.concatenate(

time: 443 us -> 648 us (1.46)
  waiting for transfers between devices: 344 us -> 523 us
  local copies, waits for them, and re-layouts: 15.5 us -> 44.8 us
  starting transfers between devices: 0.18 us -> 12.1 us
  matrix products: 34.9 us -> 26.3 us
  other arithmetic: 34.5 us -> 26.8 us
    all_to_all x0 -> x1, waiting for transfers between devices: none -> 277 us  [local(): blocks = lax.all_to_all(blocks, MP, split_axis=0, concat_axis=0)]
    all_gather x1 -> x0, waiting for transfers between devices: 125 us -> none  [local(): whole_rows = lax.all_gather(arrived, MP, axis=1, tiled=True)]
    all_gather x1, waiting for transfers between devices: 58.3 us -> 85.4 us  [sent_together(): result, at, outs = (lax.all_gather(both, axis, axis=dim, tiled=True), 0, [])]
    all_to_all x0 -> x1, local copies, waits for them, and re-layouts: none -> 16.7 us  [local(): blocks = lax.all_to_all(blocks, MP, split_axis=0, concat_axis=0)]
    all_to_all x0 -> x1, starting transfers between devices: none -> 11.8 us  [local(): blocks = lax.all_to_all(blocks, MP, split_axis=0, concat_axis=0)]
    dot_general x3, matrix products: 21.7 us -> 13.2 us  [channel_product(): lax.dot_general(weights, normed, (((1,), (1,)), ((), ())), preferred_elem...]
    convert_element_type x1 -> x0, other arithmetic: 7.47 us -> none  [normalize(): (as_float * lax.rsqrt(mean_square + norm_eps) * gain_row).astype(jnp.bflo...]
    another operation x2 -> x3, other arithmetic: 1.92 us -> 9.38 us
  transfers between devices with their start and end apart: 5 -> 5, of which waited for: 5 -> 5; matrix products, arithmetic and copies ran while one was open for 7% -> 4% of each run, Pallas kernels for 0% -> 0%
where the time goes in v1:
time: 648 us; the launch traced here: 647 us
  waiting for transfers between devices  523 us (81%)
  local copies, waits for them, and re-layouts  44.8 us (7%)
  other arithmetic  26.8 us (4%)
  matrix products  26.3 us (4%)
  between operations  14 us (2%)
  starting transfers between devices  12.1 us (2%)
    all_to_all x1, waiting for transfers between devices, local(): blocks = lax.all_to_all(blocks, MP, split_axis=0, concat_axis=0)  277 us
    reduce_scatter x2, waiting for transfers between devices, scatter_axes(): array = lax.psum_scatter(array, axis, scatter_dimension=dim, tiled=True)  152 us
    all_gather x1, waiting for transfers between devices, sent_together(): result, at, outs = (lax.all_gather(both, axis, axis=dim, tiled=True), 0, [])  85.4 us
    all_to_all x1, local copies, waits for them, and re-layouts, local(): blocks = lax.all_to_all(blocks, MP, split_axis=0, concat_axis=0)  16.7 us
    dot_general x3, matrix products, channel_product(): lax.dot_general(weights, normed, (((1,), (1,)), ((), ())), preferred_elem...  13.2 us
  transfers between devices with their start and end apart: 5, of which 5 were waited for; matrix products, arithmetic and copies ran while one was open for 4% of the time, Pallas kernels for 0%

profile of v1, /device:TPU:6, one launch (start us, length us, event | category | flops | bytes accessed | tf_op | source)
XLA Modules:
  0.0 647.3 jit_solution(18410520962318758692)
XLA Ops:
  7.2 8.6 %collective-permute-done = bf16[768,256]{1,0:T(8,128)(2,1)S(1)} collective-permute-done((bf16[768,256]{1,0:T(8,128)(2,1)}, bf16[768,256]{1,0:T(8,128)(2,1)S(1)}, u32[]{:S(2)}, u32[]{:S(2)}) %collective-permute-start) | collective-permute-done | bytes 393248 | tf_op jit(solution)/shard_map/ppermute | solution.py:18
  15.8 6.0 stack.8
  21.8 11.8 %all-to-all-start = ((bf16[32,768,256]{2,1,0:T(8,128)(2,1)}), bf16[32,768,256]{2,1,0:T(8,128)(2,1)}, u32[]{:S(2)}, u32[]{:S(2)}) async-start(bf16[32,768,256]{2,1,0:T(8,128)(2,1)} %stack.8), calls=%async_computation | async-start | bytes 25165824 | tf_op jit(solution)/shard_map/all_to_all | solution.py:91
  33.8 277.0 %all-to-all-done = bf16[32,768,256]{2,1,0:T(8,128)(2,1)} async-done(((bf16[32,768,256]{2,1,0:T(8,128)(2,1)}), bf16[32,768,256]{2,1,0:T(8,128)(2,1)}, u32[]{:S(2)}, u32[]{:S(2)}) %all-to-all-start) | async-done | bytes 12582944 | tf_op jit(solution)/shard_map/all_to_all | solution.py:91
  310.8 16.7 %copy.27 = bf16[32,768,256]{1,2,0:T(8,128)(2,1)} copy(bf16[32,768,256]{2,1,0:T(8,128)(2,1)} %all-to-all-done) | data formatting | bytes 25165824 | tf_op jit(solution)/shard_map/all_to_all | solution.py:91
  327.4 7.4 %multiply_reduce_fusion = f32[768]{0:T(1024)S(1)} fusion(bf16[32,768,256]{1,2,0:T(8,128)(2,1)} %copy.27), kind=kLoop, calls=%fused_computation.2 | loop fusion | flops 18873600 | bytes 12585984 | tf_op jit(solution)/shard_map/reduce_sum | solution.py:66
  334.9 7.5 %multiply_convert_fusion = bf16[32,768,256]{1,2,0:T(8,128)(2,1)S(1)} fusion(f32[32,256]{1,0:T(8,128)S(1)} %reshape.328, f32[768]{0:T(1024)S(1)} %add_rsqrt_fusion, bf16[32,768,256]{1,2,0:T(8,128)(2,1)} %copy.27), kind=kLoop, calls=%fused_computation.1 | loop fusion | flops 25165824 | bytes 25201664 | tf_op jit(solution)/shard_map/convert.7
  342.3 2.2 fusion.13
  344.5 2.2 copy-done.2
  346.8 2.2 convolution_bitcast_fusion
  350.6 8.8 %fusion.9 = f32[256,768]{1,0:T(8,128)S(1)} fusion(bf16[768,8192]{0,1:T(8,128)(2,1)} %bitcast.59, bf16[1,256,8192]{2,1,0:T(8,128)(2,1)} %param.8), kind=kOutput, calls=%fused_computation.16 | convolution fusion | flops 3221225472 | bytes 17563648 | tf_op jit(solution)/shard_map/dot_general | solution.py:72
  360.6 1.7 fusion.23
  362.9 85.4 %all-gather.2.cloned.1.call-done = bf16[1024,1536]{1,0:T(8,128)(2,1)} async-done(((bf16[32,1536]{1,0:T(8,128)(2,1)}), bf16[1024,1536]{1,0:T(8,128)(2,1)}) %all-gather.2.cloned.1.call-update) | async-done | bytes 3145744 | tf_op jit(solution)/shard_map/all_gather | solution.py:23
  448.3 3.3 fusion.45
  451.5 4.5 reshape.325
  459.9 3.8 fusion.48
  463.6 3.0 fusion.12
  467.2 6.3 convolution_convert_fusion
  473.7 113.6 %reduce-scatter.3.cloned.1.call-done = bf16[192,8192]{1,0:T(8,128)(2,1)} async-done(((bf16[768,8192]{1,0:T(8,128)(2,1)}), bf16[192,8192]{1,0:T(8,128)(2,1)}) %reduce-scatter.3.cloned.1.call-update) | async-done | bytes 3145744 | tf_op jit(solution)/shard_map/reduce_scatter | solution.py:32
  587.2 7.1 %convert_element_type.100 = f32[32,768,256]{1,2,0:T(8,128)S(1)} convert(bf16[32,768,256]{1,2,0:T(8,128)(2,1)} %copy.27) | non-fusion elementwise | flops 6291456 | bytes 37748736 | tf_op jit(solution)/shard_map/convert_element_type | solution.py:65
  594.4 3.1 constant_dynamic-slice_fusion
  597.5 2.8 copy.47
  600.3 38.7 %reduce-scatter.5.cloned.1.call-done = bf16[24,8192]{1,0:T(8,128)(2,1)} async-done(((bf16[192,8192]{1,0:T(8,128)(2,1)}), bf16[24,8192]{1,0:T(8,128)(2,1)}) %reduce-scatter.5.cloned.1.call-update) | async-done | bytes 393232 | tf_op jit(solution)/shard_map/reduce_scatter | solution.py:32
  639.0 1.8 fusion.26
  (42 shorter events, 7.9 us)
Async XLA Ops:
  7.2 335.2 %copy-start = (bf16[1,32,8192]{2,1,0:T(8,128)(2,1)S(1)}, bf16[1,32,8192]{2,1,0:T(8,128)(2,1)}, u32[]{:S(2)}) copy-start(bf16[1,32,8192]{2,1,0:T(8,128)(2,1)} %param.10) | copy-start | bytes 1572868
  7.2 8.6 %collective-permute-start = (bf16[768,256]{1,0:T(8,128)(2,1)}, bf16[768,256]{1,0:T(8,128)(2,1)S(1)}, u32[]{:S(2)}, u32[]{:S(2)}) collective-permute-start(bf16[768,256]{1,0:T(8,128)(2,1)} %bitcast.63), channel_id=1, source_target_pairs={{224,0},{0,32},{32,64},{64,96},{96,128},{128,160},{160,192},{192,2... | collective-permute-start | bytes 1179656 | tf_op jit(solution)/shard_map/ppermute | solution.py:18
  21.8 11.8 %copy-start.5 = (bf16[1,8192]{1,0:T(2,128)(2,1)S(1)}, bf16[1,8192]{1,0:T(2,128)(2,1)}, u32[]{:S(2)}) copy-start(bf16[1,8192]{1,0:T(2,128)(2,1)} %param.7) | copy-start | bytes 49156
  21.8 289.0 %all-to-all-start = ((bf16[32,768,256]{2,1,0:T(8,128)(2,1)}), bf16[32,768,256]{2,1,0:T(8,128)(2,1)}, u32[]{:S(2)}, u32[]{:S(2)}) async-start(bf16[32,768,256]{2,1,0:T(8,128)(2,1)} %stack.8), calls=%async_computation | async-start | bytes 25165824 | tf_op jit(solution)/shard_map/all_to_all | solution.py:91
  33.6 414.7 %all-gather.2.cloned.1.call-start = ((), (), s32[]{:S(2)}) async-start(), calls=%async_computation.3 | async-start | bytes 3244032 | tf_op jit(solution)/shard_map/all_gather | solution.py:23
  342.3 4.5 copy-start.2
  342.3 4.5 copy-start.4
  350.2 237.0 %reduce-scatter.3.cloned.1.call-start = ((), (), s32[]{:S(2)}) async-start(), calls=%async_computation.4 | async-start | bytes 15728640 | tf_op jit(solution)/shard_map/reduce_scatter | solution.py:32
  463.6 3.6 copy-start.3
  473.6 165.4 %reduce-scatter.5.cloned.1.call-start = ((), (), s32[]{:S(2)}) async-start(), calls=%async_computation.5 | async-start | bytes 3538944 | tf_op jit(solution)/shard_map/reduce_scatter | solution.py:32
  594.4 46.4 %copy-start.1 = (bf16[1,32,8192]{2,1,0:T(8,128)(2,1)S(1)}, bf16[1,32,8192]{2,1,0:T(8,128)(2,1)}, u32[]{:S(2)}) copy-start(bf16[1,32,8192]{2,1,0:T(8,128)(2,1)} %param.10) | copy-start | bytes 1572868
Sparse Core Ops, SparseCore 0:
  350.3 97.9 all-gather.1
  473.7 113.4 reduce-scatter.2
  590.4 48.5 reduce-scatter.4
